TPU v7x, 128 devices: a whole 4x4x4 slice. The times are simulated.
128 devices in a mesh: gx: 4 (over z_hi, core), gy: 4 (over x), gz: 8 (over y, z_lo).
Axes of the slice: x: 4, y: 4, z: 4 (z_hi: 2, z_lo: 2; z = z_hi * 2 + z_lo), core: 2. Of those that a mesh axis runs over, the one named last changes fastest.
Arguments:
- x_a: bfloat16 [32, 8, 64, 1024], P(None, 'gx', 'gy', 'gz'), may hold values from -12 to 12
- x_b: bfloat16 [32, 8, 64, 1024], P(None, 'gx', 'gy', 'gz'), may hold values from -12 to 12
- w_first: bfloat16 [3, 3, 3, 32, 32], replicated, may hold values from -0.21875 to 0.21875
- w_second: bfloat16 [3, 3, 3, 32, 32], replicated, may hold values from -0.21875 to 0.21875
- gain_first: float32 [32], replicated, may hold values from 0.1 to 1.9
- bias_first: float32 [32], replicated, may hold values from -2 to 2
- gain_second: float32 [32], replicated, may hold values from 0.1 to 1.9
- bias_second: float32 [32], replicated, may hold values from -2 to 2
- grad_out: bfloat16 [32, 8, 64, 1024], P(None, 'gx', 'gy', 'gz'), may hold values from -6 to 6
Outputs:
- y_a: bfloat16 [32, 8, 64, 1024], P(None, 'gx', 'gy', 'gz')
- dx_b: bfloat16 [32, 8, 64, 1024], P(None, 'gx', 'gy', 'gz')
- grad_w_first: float32 [3, 3, 3, 32, 32], replicated
- grad_w_second: float32 [3, 3, 3, 32, 32], replicated
- grad_norm: float32 [4, 32], replicated
All inputs are finite; a program needn't handle non-finite values.
Results may differ from a plain program's by a relative error of at most 0.0063.
Values may be sent and summed in bfloat16 or wider, within the bound.
A program may use at most 128 MiB of HBM per device.

v0:
```python
import functools
import math
import jax
import jax.numpy as jnp
from jax import lax
from jax.sharding import Mesh
from jax.sharding import PartitionSpec as P

GX_GY_GZ = ("gx_0", "gx_1", "gy", "gz_0", "gz_1")
GX = ("gx_0", "gx_1")
GZ = ("gz_0", "gz_1")
EPSILON = 1e-05


def by_axis(value, axes):
    return functools.reduce(lax.psum, axes, value)


def extended(block, sides, width):
    for axis, dim in sides:
        count = lax.axis_size(axis)
        forward = [(i, i + 1) for i in range(count - 1)]
        backward = [(target, source) for source, target in forward]
        low = lax.ppermute(
            lax.slice_in_dim(block, block.shape[dim] - width, None, axis=dim), axis, forward
        )
        high = lax.ppermute(lax.slice_in_dim(block, 0, width, axis=dim), axis, backward)
        block = jnp.concatenate([low, block, high], axis=dim)
    return block


def spread(values):
    return values[:, None, None, None]


def silu_slope(value):
    sigma = jax.nn.sigmoid(value)
    return sigma * (1.0 + value * (1.0 - sigma))


def convolve(padded, weight):
    in_chan = padded.shape[0]
    out_chan = weight.shape[3]
    span_x = padded.shape[1] - 2
    span_y = padded.shape[2] - 2
    span_z = padded.shape[3] - 2
    total = jnp.zeros((out_chan, span_x * span_y * span_z), jnp.float32)
    for shift_x in range(3):
        for shift_y in range(3):
            pieces = [
                padded[
                    :,
                    shift_x : shift_x + span_x,
                    shift_y : shift_y + span_y,
                    shift_z : shift_z + span_z,
                ]
                for shift_z in range(3)
            ]
            stacked = jnp.concatenate(pieces, axis=0).reshape(3 * in_chan, -1)
            matrix = weight[shift_x, shift_y].transpose(1, 0, 2).reshape(out_chan, 3 * in_chan)
            total = total + jnp.dot(matrix, stacked, preferred_element_type=jnp.float32)
    return total.reshape(out_chan, span_x, span_y, span_z)


def kernel_grad(padded, upstream):
    in_chan = padded.shape[0]
    out_chan = upstream.shape[0]
    span_x, span_y, span_z = (upstream.shape[1], upstream.shape[2], upstream.shape[3])
    flat = upstream.reshape(out_chan, -1)
    rows = []
    for shift_x in range(3):
        for shift_y in range(3):
            pieces = [
                padded[
                    :,
                    shift_x : shift_x + span_x,
                    shift_y : shift_y + span_y,
                    shift_z : shift_z + span_z,
                ]
                for shift_z in range(3)
            ]
            stacked = jnp.concatenate(pieces, axis=0).reshape(3 * in_chan, -1)
            product = lax.dot_general(
                flat, stacked, (((1,), (1,)), ((), ())), preferred_element_type=jnp.float32
            )
            rows.append(product.reshape(out_chan, 3, in_chan).transpose(1, 0, 2))
    return jnp.stack(rows).reshape(3, 3, 3, out_chan, in_chan)


def flipped(weight):
    return jnp.flip(weight, (0, 1, 2)).transpose(0, 1, 2, 4, 3)


def statistics(blocks, voxels):
    local_sums = jnp.stack([jnp.sum(block, axis=(1, 2, 3)) for block in blocks])
    local_squares = jnp.stack([jnp.sum(jnp.square(block), axis=(1, 2, 3)) for block in blocks])
    sums, squares = (by_axis(local_sums, GX_GY_GZ), by_axis(local_squares, GX_GY_GZ))
    means = sums / voxels
    variance = squares / voxels - means * means
    return (means, lax.rsqrt(variance + EPSILON))


def normalize(block, means, scales, gain, bias):
    normed = (block - spread(means)) * spread(scales)
    return (normed, spread(gain) * normed + spread(bias))


def backward_layer(upstream, preact, normed, scales, gain, voxels):
    slope = upstream * silu_slope(preact)
    sum_d, sum_dx = (
        by_axis(jnp.sum(slope, axis=(1, 2, 3)), GX_GY_GZ),
        by_axis(jnp.sum(slope * normed, axis=(1, 2, 3)), GX_GY_GZ),
    )
    delta = spread(gain * scales) * (
        slope - spread(sum_d / voxels) - normed * spread(sum_dx / voxels)
    )
    return (delta.astype(jnp.bfloat16), sum_d, sum_dx)


def body(x_a, x_b, w_first, w_second, gain_first, bias_first, gain_second, bias_second, grad_out):
    rows_x, rows_y, rows_z = (x_a.shape[1], x_a.shape[2], x_a.shape[3])
    voxels = float(
        rows_x * rows_y * rows_z * lax.axis_size(GX) * lax.axis_size("gy") * lax.axis_size(GZ)
    )
    factor = 1.0 / math.sqrt(voxels)
    volumes = jnp.stack([x_a, x_b])
    padded = extended(volumes, ((GX, 2), ("gy", 3), (GZ, 4)), 1)
    first = [convolve(padded[member], w_first) for member in range(2)]
    means, scales = statistics(first, voxels)
    hidden = []
    for member in range(2):
        normed, preact = normalize(
            first[member], means[member], scales[member], gain_first, bias_first
        )
        hidden.append((preact * jax.nn.sigmoid(preact)).astype(jnp.bfloat16))
    hidden_all = extended(jnp.stack(hidden), ((GX, 2), ("gy", 3), (GZ, 4)), 1)
    hidden_pads = [hidden_all[0], hidden_all[1]]
    input_pad_b = padded[1]
    scale_one = scales[1]
    second = [convolve(hidden_pads[member], w_second) for member in range(2)]
    means_two, scales_two = statistics(second, voxels)
    normed_a, preact_a = normalize(second[0], means_two[0], scales_two[0], gain_second, bias_second)
    y_a = (preact_a * jax.nn.sigmoid(preact_a)).astype(jnp.bfloat16)
    norm_two, pre_two = normalize(second[1], means_two[1], scales_two[1], gain_second, bias_second)
    delta_two, sum_d2, sum_x2 = backward_layer(
        grad_out.astype(jnp.float32), pre_two, norm_two, scales_two[1], gain_second, voxels
    )
    local_second = kernel_grad(hidden_pads[1], delta_two) * factor
    grad_w_second = lax.psum(local_second, GX_GY_GZ)
    delta_pad_two = extended(delta_two, ((GX, 1), ("gy", 2), (GZ, 3)), 1)
    upstream_one = convolve(delta_pad_two, flipped(w_second))
    delta_one, sum_d1, sum_x1 = backward_layer(
        upstream_one, preact, normed, scale_one, gain_first, voxels
    )
    local_first = kernel_grad(input_pad_b, delta_one) * factor
    delta_pad_one = extended(delta_one, ((GX, 1), ("gy", 2), (GZ, 3)), 1)
    dx_b = convolve(delta_pad_one, flipped(w_first)).astype(jnp.bfloat16)
    grad_w_first = lax.psum(local_first, GX_GY_GZ)
    grad_norm = jnp.stack([sum_x1, sum_d1, sum_x2, sum_d2]) * factor
    return (y_a, dx_b, grad_w_first, grad_w_second, grad_norm)


def solution(mesh):
    torus = Mesh(
        mesh.devices.reshape(2, 2, mesh.shape["gy"], 4, 2), ("gx_0", "gx_1", "gy", "gz_0", "gz_1")
    )
    in_specs = (
        P(None, GX, "gy", GZ),
        P(None, GX, "gy", GZ),
        P(),
        P(),
        P(),
        P(),
        P(),
        P(),
        P(None, GX, "gy", GZ),
    )
    out_specs = (P(None, GX, "gy", GZ), P(None, GX, "gy", GZ), P(), P(), P())
    return jax.shard_map(body, mesh=torus, in_specs=in_specs, out_specs=out_specs, check_vma=False)
```

profile of v0, /device:TPU:1, one launch (start us, length us, event | category | flops | bytes accessed | tf_op | source)
XLA Modules:
  0.0 573.7 jit_solution(8080305644700961799)
XLA Ops:
  8.4 6.9 %collective-permute-start = (bf16[2,32,1,16,128]{4,3,2,1,0:T(8,128)(2,1)S(1)}, bf16[2,32,1,16,128]{4,3,2,1,0:T(8,128)(2,1)S(1)}, u32[]{:S(2)}, u32[]{:S(2)}) collective-permute-start(bf16[2,32,1,16,128]{4,3,2,1,0:T(8,128)(2,1)S(1)} %get-tuple-element.259), channel_id=1, source_target_pairs={{0,32},{32,64},{64,96},{1,33},{33,65},{65,97},{2,34},{34,66},{66,9... | collective-permute-start | bytes 786440 | tf_op jit(solution)/shard_map/ppermute | solution.py:24
  15.3 1.9 collective-permute-start.1
  18.6 5.9 %collective-permute-done.1 = bf16[2,32,1,16,128]{4,3,2,1,0:T(8,128)(2,1)S(1)} collective-permute-done((bf16[2,32,1,16,128]{4,3,2,1,0:T(8,128)(2,1)S(1)}, bf16[2,32,1,16,128]{4,3,2,1,0:T(8,128)(2,1)S(1)}, u32[]{:S(2)}, u32[]{:S(2)}) %collective-permute-start.1) | collective-permute-done | bytes 262176 | tf_op jit(solution)/shard_map/ppermute | solution.py:27
  24.7 3.7 copy.460
  29.6 3.1 collective-permute-start.2
  36.1 3.8 collective-permute-done.3
  39.9 6.2 %pad_maximum_fusion = bf16[2,32,4,18,128]{1,2,4,3,0:T(4,128)(2,1)S(1)} fusion(bf16[2,32,4,1,128]{1,2,4,3,0:T(4,128)(2,1)S(1)} %collective-permute-done.3, bf16[2,32,4,16,128]{1,2,4,3,0:T(4,128)(2,1)} %copy.460, bf16[2,32,4,1,128]{1,2,4,3,0:T(4,128)(2,1)S(1)} %collective-permute-done.2), kind=kLoop, calls=%fused_computation | loop fusion | flops 1179648 | bytes 2359296 | tf_op jit(solution)/shard_map/concatenate | solution.py:28
  46.1 2.2 copy-done
  48.3 3.3 collective-permute-start.4
  58.7 6.3 %copy.464 = bf16[2,32,4,18,128]{4,1,3,2,0:T(8,128)(2,1)S(1)} copy(bf16[2,32,4,18,128]{1,2,4,3,0:T(4,128)(2,1)} %copy-done) | data formatting | bytes 2359296 | tf_op jit(solution)/shard_map/concatenate | solution.py:28
  66.0 1.7 copy.463
  72.2 3.3 fusion.175
  99.3 5.3 all-reduce.20
  104.6 2.5 all-reduce.16
  107.0 7.2 %all-reduce.8 = (f32[2,32]{1,0:T(2,128)S(1)}, f32[2,32]{1,0:T(2,128)S(1)}) all-reduce(f32[2,32]{1,0:T(2,128)S(1)} %get-tuple-element.61, f32[2,32]{1,0:T(2,128)S(1)} %get-tuple-element.62), channel_id=1, replica_groups=mesh['gx_0'=2,'gx_1'=2,'gy'=4,'gz_0'=4,'gz_1'=2] {'gy'}, use_global_device_ids=true, to_apply=%region_11.0 | all-reduce | flops 128 | bytes 1024 | tf_op jit(solution)/shard_map/psum | solution.py:16
  114.2 10.4 %all-reduce.4 = (f32[2,32]{1,0:T(2,128)S(1)}, f32[2,32]{1,0:T(2,128)S(1)}) all-reduce(f32[2,32]{1,0:T(2,128)S(1)} %get-tuple-element.45, f32[2,32]{1,0:T(2,128)S(1)} %get-tuple-element.46), channel_id=1, replica_groups=mesh['gx_0'=2,'gx_1'=2,'gy'=4,'gz_0'=4,'gz_1'=2] {'gz_0'}, use_global_device_ids=true, to_apply=%region_12.0 | all-reduce | flops 128 | bytes 1024 | tf_op jit(solution)/shard_map/psum | solution.py:16
  124.6 3.8 all-reduce.12
  130.7 10.1 %collective-permute-start.6 = (bf16[2,32,1,16,128]{4,3,2,1,0:T(8,128)(2,1)S(1)}, bf16[2,32,1,16,128]{4,3,2,1,0:T(8,128)(2,1)S(1)}, u32[]{:S(2)}, u32[]{:S(2)}) collective-permute-start(bf16[2,32,1,16,128]{4,3,2,1,0:T(8,128)(2,1)S(1)} %get-tuple-element.257), channel_id=1, source_target_pairs={{0,32},{32,64},{64,96},{1,33},{33,65},{65,97},{2,34},{34,66},{66,9... | collective-permute-start | bytes 786440 | tf_op jit(solution)/shard_map/ppermute | solution.py:24
  140.7 1.9 collective-permute-start.7
  144.0 5.9 %collective-permute-done.7 = bf16[2,32,1,16,128]{4,3,2,1,0:T(8,128)(2,1)S(1)} collective-permute-done((bf16[2,32,1,16,128]{4,3,2,1,0:T(8,128)(2,1)S(1)}, bf16[2,32,1,16,128]{4,3,2,1,0:T(8,128)(2,1)S(1)}, u32[]{:S(2)}, u32[]{:S(2)}) %collective-permute-start.7) | collective-permute-done | bytes 262176 | tf_op jit(solution)/shard_map/ppermute | solution.py:27
  151.0 5.6 copy.493
  156.7 2.1 fusion.165
  158.7 2.2 collective-permute-start.8
  168.4 6.3 %pad_maximum_fusion.1 = bf16[2,32,4,18,128]{1,2,4,3,0:T(4,128)(2,1)S(1)} fusion(bf16[2,32,4,1,128]{1,2,4,3,0:T(4,128)(2,1)} %collective-permute-done.9, bf16[2,32,4,16,128]{1,2,4,3,0:T(4,128)(2,1)} %copy.493, bf16[2,32,4,1,128]{1,2,4,3,0:T(4,128)(2,1)S(1)} %collective-permute-done.8), kind=kLoop, calls=%fused_computation.1 | loop fusion | flops 1179648 | bytes 2359296 | tf_op jit(solution)/shard_map/concatenate | solution.py:28
  174.7 2.2 copy-done.1
  176.8 1.7 collective-permute-start.10
  182.4 2.2 dot_general.394
  192.0 7.1 %copy.497 = bf16[2,32,4,18,128]{4,1,3,2,0:T(8,128)(2,1)} copy(bf16[2,32,4,18,128]{1,2,4,3,0:T(4,128)(2,1)} %copy-done.1) | data formatting | bytes 2359296 | tf_op jit(solution)/shard_map/concatenate | solution.py:28
  201.1 2.6 pad_maximum_fusion.3
  203.8 1.8 fusion.174
  205.7 3.1 fusion.173
  210.0 3.0 fusion.171
  240.4 2.2 dot_general.408
  246.5 2.2 dot_general.404
  254.1 5.3 all-reduce.19
  259.4 2.5 all-reduce.15
  261.9 8.3 %all-reduce.7 = (f32[2,32]{1,0:T(2,128)S(1)}, f32[2,32]{1,0:T(2,128)S(1)}) all-reduce(f32[2,32]{1,0:T(2,128)S(1)} %get-tuple-element.59, f32[2,32]{1,0:T(2,128)S(1)} %get-tuple-element.60), channel_id=1, replica_groups=mesh['gx_0'=2,'gx_1'=2,'gy'=4,'gz_0'=4,'gz_1'=2] {'gy'}, use_global_device_ids=true, to_apply=%region_25.0 | all-reduce | flops 128 | bytes 1024 | tf_op jit(solution)/shard_map/psum | solution.py:16
  270.2 8.6 %all-reduce.3 = (f32[2,32]{1,0:T(2,128)S(1)}, f32[2,32]{1,0:T(2,128)S(1)}) all-reduce(f32[2,32]{1,0:T(2,128)S(1)} %get-tuple-element.43, f32[2,32]{1,0:T(2,128)S(1)} %get-tuple-element.44), channel_id=1, replica_groups=mesh['gx_0'=2,'gx_1'=2,'gy'=4,'gz_0'=4,'gz_1'=2] {'gz_0'}, use_global_device_ids=true, to_apply=%region_26.0 | all-reduce | flops 128 | bytes 1024 | tf_op jit(solution)/shard_map/psum | solution.py:16
  278.8 3.8 all-reduce.11
  282.8 1.9 fusion.162
  284.6 5.3 all-reduce.18
  289.9 8.6 %all-reduce.14 = (f32[32]{0:T(128)S(1)}, f32[32]{0:T(128)S(1)}) all-reduce(f32[32]{0:T(128)S(1)} %get-tuple-element.65, f32[32]{0:T(128)S(1)} %get-tuple-element.66), channel_id=1, replica_groups=mesh['gx_0'=2,'gx_1'=2,'gy'=4,'gz_0'=4,'gz_1'=2] {'gx_1'}, use_global_device_ids=true, to_apply=%region_36.0 | all-reduce | flops 64 | bytes 512 | tf_op jit(solution)/shard_map/psum | solution.py:16
  298.5 6.1 %all-reduce.6 = (f32[32]{0:T(128)S(1)}, f32[32]{0:T(128)S(1)}) all-reduce(f32[32]{0:T(128)S(1)} %get-tuple-element.57, f32[32]{0:T(128)S(1)} %get-tuple-element.58), channel_id=1, replica_groups=mesh['gx_0'=2,'gx_1'=2,'gy'=4,'gz_0'=4,'gz_1'=2] {'gy'}, use_global_device_ids=true, to_apply=%region_37.0 | all-reduce | flops 64 | bytes 512 | tf_op jit(solution)/shard_map/psum | solution.py:16
  304.6 6.2 %all-reduce.2 = (f32[32]{0:T(128)S(1)}, f32[32]{0:T(128)S(1)}) all-reduce(f32[32]{0:T(128)S(1)} %get-tuple-element.41, f32[32]{0:T(128)S(1)} %get-tuple-element.42), channel_id=1, replica_groups=mesh['gx_0'=2,'gx_1'=2,'gy'=4,'gz_0'=4,'gz_1'=2] {'gz_0'}, use_global_device_ids=true, to_apply=%region_38.0 | all-reduce | flops 64 | bytes 512 | tf_op jit(solution)/shard_map/psum | solution.py:16
  310.7 3.9 all-reduce.10
  318.2 9.4 %collective-permute-start.12 = (bf16[32,1,16,128]{3,0,2,1:T(8,128)(2,1)}, bf16[32,1,16,128]{3,0,2,1:T(8,128)(2,1)S(1)}, u32[]{:S(2)}, u32[]{:S(2)}) collective-permute-start(bf16[32,1,16,128]{3,0,2,1:T(8,128)(2,1)} %get-tuple-element.269), channel_id=1, source_target_pairs={{0,32},{32,64},{64,96},{1,33},{33,65},{65,97},{2,34},{34,66},{66,9... | collective-permute-start | bytes 393224 | tf_op jit(solution)/shard_map/ppermute | solution.py:24
  327.6 2.1 collective-permute-start.13
  336.4 3.4 collective-permute-start.14
  342.8 1.7 collective-permute-done.15
  348.0 4.0 collective-permute-start.16
  355.0 2.2 maximum_maximum_fusion
  366.1 5.4 all-reduce.17
  371.5 5.9 %all-reduce.13 = (f32[32]{0:T(128)S(1)}, f32[32]{0:T(128)S(1)}) all-reduce(f32[32]{0:T(128)S(1)} %get-tuple-element.63, f32[32]{0:T(128)S(1)} %get-tuple-element.64), channel_id=1, replica_groups=mesh['gx_0'=2,'gx_1'=2,'gy'=4,'gz_0'=4,'gz_1'=2] {'gx_1'}, use_global_device_ids=true, to_apply=%region_48.49 | all-reduce | flops 64 | bytes 512 | tf_op jit(solution)/shard_map/psum | solution.py:16
  377.4 6.1 %all-reduce.5 = (f32[32]{0:T(128)S(1)}, f32[32]{0:T(128)S(1)}) all-reduce(f32[32]{0:T(128)S(1)} %get-tuple-element.55, f32[32]{0:T(128)S(1)} %get-tuple-element.56), channel_id=1, replica_groups=mesh['gx_0'=2,'gx_1'=2,'gy'=4,'gz_0'=4,'gz_1'=2] {'gy'}, use_global_device_ids=true, to_apply=%region_49.50 | all-reduce | flops 64 | bytes 512 | tf_op jit(solution)/shard_map/psum | solution.py:16
  383.5 10.0 %all-reduce.1 = (f32[32]{0:T(128)S(1)}, f32[32]{0:T(128)S(1)}) all-reduce(f32[32]{0:T(128)S(1)} %get-tuple-element.39, f32[32]{0:T(128)S(1)} %get-tuple-element.40), channel_id=1, replica_groups=mesh['gx_0'=2,'gx_1'=2,'gy'=4,'gz_0'=4,'gz_1'=2] {'gz_0'}, use_global_device_ids=true, to_apply=%region_50.51 | all-reduce | flops 64 | bytes 512 | tf_op jit(solution)/shard_map/psum | solution.py:16
  393.5 3.8 all-reduce.9
  398.3 10.4 %collective-permute-start.18 = (bf16[32,1,16,128]{3,0,2,1:T(8,128)(2,1)S(1)}, bf16[32,1,16,128]{3,0,2,1:T(8,128)(2,1)S(1)}, u32[]{:S(2)}, u32[]{:S(2)}) collective-permute-start(bf16[32,1,16,128]{3,0,2,1:T(8,128)(2,1)S(1)} %get-tuple-element.264), channel_id=1, source_target_pairs={{0,32},{32,64},{64,96},{1,33},{33,65},{65,97},{2,34},{34,66},{66,9... | collective-permute-start | bytes 393224 | tf_op jit(solution)/shard_map/ppermute | solution.py:24
  408.7 2.3 collective-permute-start.19
  417.4 3.6 collective-permute-start.20
  423.0 2.8 collective-permute-done.21
  428.7 4.0 collective-permute-start.22
  444.8 118.3 %all-reduce.23.cloned.1.call-done = (f32[3,3,3,32,32]{4,3,2,1,0:T(8,128)}, f32[3,3,3,32,32]{4,3,2,1,0:T(8,128)}) async-done(((f32[3,3,3,32,32]{4,3,2,1,0:T(8,128)}, f32[3,3,3,32,32]{4,3,2,1,0:T(8,128)}), (f32[3,3,3,32,32]{4,3,2,1,0:T(8,128)}, f32[3,3,3,32,32]{4,3,2,1,0:T(8,128)})) %all-reduce.23.cloned.1.call-update) | async-done | bytes 221200 | tf_op jit(solution)/shard_map/psum | solution.py:158
  563.0 1.8 copy.917
  564.8 1.8 copy.918
  (639 shorter events, 157.5 us)
Async XLA Ops:
  7.2 17.4 %copy-start.99 = (bf16[32,2,16,128]{3,2,1,0:T(8,128)(2,1)S(1)}, bf16[32,2,16,128]{3,2,1,0:T(8,128)(2,1)}, u32[]{:S(2)}) copy-start(bf16[32,2,16,128]{3,2,1,0:T(8,128)(2,1)} %param.10) | copy-start | bytes 786436
  7.2 17.3 %copy-start.98 = (bf16[32,2,16,128]{3,2,1,0:T(8,128)(2,1)S(1)}, bf16[32,2,16,128]{3,2,1,0:T(8,128)(2,1)}, u32[]{:S(2)}) copy-start(bf16[32,2,16,128]{3,2,1,0:T(8,128)(2,1)} %param.9) | copy-start | bytes 786436
  7.2 555.8 %all-reduce.23.cloned.1.call-start = ((), (), s32[]{:S(2)}) async-start(), calls=%async_computation | async-start | bytes 1769472 | tf_op jit(solution)/shard_map/psum | solution.py:158
  8.4 10.2 %collective-permute-start = (bf16[2,32,1,16,128]{4,3,2,1,0:T(8,128)(2,1)S(1)}, bf16[2,32,1,16,128]{4,3,2,1,0:T(8,128)(2,1)S(1)}, u32[]{:S(2)}, u32[]{:S(2)}) collective-permute-start(bf16[2,32,1,16,128]{4,3,2,1,0:T(8,128)(2,1)S(1)} %get-tuple-element.259), channel_id=1, source_target_pairs={{0,32},{32,64},{64,96},{1,33},{33,65},{65,97},{2,34},{34,66},{66,9... | collective-permute-start | bytes 786440 | tf_op jit(solution)/shard_map/ppermute | solution.py:24
  15.3 9.2 %collective-permute-start.1 = (bf16[2,32,1,16,128]{4,3,2,1,0:T(8,128)(2,1)S(1)}, bf16[2,32,1,16,128]{4,3,2,1,0:T(8,128)(2,1)S(1)}, u32[]{:S(2)}, u32[]{:S(2)}) collective-permute-start(bf16[2,32,1,16,128]{4,3,2,1,0:T(8,128)(2,1)S(1)} %get-tuple-element.260), channel_id=1, source_target_pairs={{32,0},{64,32},{96,64},{33,1},{65,33},{97,65},{34,2},{66,34},{98,6... | collective-permute-start | bytes 786440 | tf_op jit(solution)/shard_map/ppermute | solution.py:27
  24.7 9.4 %copy-start.101 = (bf16[3,3,3,32,32]{4,3,2,1,0:T(8,128)(2,1)S(1)}, bf16[3,3,3,32,32]{4,3,2,1,0:T(8,128)(2,1)}, u32[]{:S(2)}) copy-start(bf16[3,3,3,32,32]{4,3,2,1,0:T(8,128)(2,1)} %param.12) | copy-start | bytes 165892
  29.6 6.4 %collective-permute-start.2 = (bf16[2,32,4,1,128]{1,2,4,3,0:T(4,128)(2,1)S(1)}, bf16[2,32,4,1,128]{1,2,4,3,0:T(4,128)(2,1)S(1)}, u32[]{:S(2)}, u32[]{:S(2)}) collective-permute-start(bf16[2,32,4,1,128]{1,2,4,3,0:T(4,128)(2,1)S(1)} %get-tuple-element.79), channel_id=1, source_target_pairs={{0,8},{8,16},{16,24},{1,9},{9,17},{17,25},{2,10},{10,18},{18,26},{... | collective-permute-start | bytes 196616 | tf_op jit(solution)/shard_map/ppermute | solution.py:24
  32.8 7.1 %collective-permute-start.3 = (bf16[2,32,4,1,128]{1,2,4,3,0:T(4,128)(2,1)S(1)}, bf16[2,32,4,1,128]{1,2,4,3,0:T(4,128)(2,1)S(1)}, u32[]{:S(2)}, u32[]{:S(2)}) collective-permute-start(bf16[2,32,4,1,128]{1,2,4,3,0:T(4,128)(2,1)S(1)} %get-tuple-element.80), channel_id=1, source_target_pairs={{8,0},{16,8},{24,16},{9,1},{17,9},{25,17},{10,2},{18,10},{26,18},{... | collective-permute-start | bytes 196616 | tf_op jit(solution)/shard_map/ppermute | solution.py:27
  34.8 18.0 %copy-start.100 = (bf16[3,3,3,32,32]{4,3,2,1,0:T(8,128)(2,1)S(1)}, bf16[3,3,3,32,32]{4,3,2,1,0:T(8,128)(2,1)}, u32[]{:S(2)}) copy-start(bf16[3,3,3,32,32]{4,3,2,1,0:T(8,128)(2,1)} %param.11) | copy-start | bytes 165892
  48.3 17.7 %collective-permute-start.4 = (bf16[2,32,4,18,1]{1,2,4,3,0:T(4,128)(2,1)S(1)}, bf16[2,32,4,18,1]{1,2,4,3,0:T(4,128)(2,1)}, u32[]{:S(2)}, u32[]{:S(2)}) collective-permute-start(bf16[2,32,4,18,1]{1,2,4,3,0:T(4,128)(2,1)S(1)} %get-tuple-element.75), channel_id=1, source_target_pairs={{0,1},{1,2},{2,3},{3,4},{4,5},{5,6},{6,7},{8,9},{9,10},{10,11},{11... | collective-permute-start | bytes 27656 | tf_op jit(solution)/shard_map/ppermute | solution.py:24
  51.5 13.5 %collective-permute-start.5 = (bf16[2,32,4,18,1]{1,2,4,3,0:T(4,128)(2,1)S(1)}, bf16[2,32,4,18,1]{1,2,4,3,0:T(4,128)(2,1)S(1)}, u32[]{:S(2)}, u32[]{:S(2)}) collective-permute-start(bf16[2,32,4,18,1]{1,2,4,3,0:T(4,128)(2,1)S(1)} %get-tuple-element.76), channel_id=1, source_target_pairs={{1,0},{2,1},{3,2},{4,3},{5,4},{6,5},{7,6},{9,8},{10,9},{11,10},{12... | collective-permute-start | bytes 27656 | tf_op jit(solution)/shard_map/ppermute | solution.py:27
  80.9 5.1 copy-start.4
  81.7 3.4 copy-start.7
  86.7 43.3 %copy-start.21 = (f32[4,8,32,128]{3,2,1,0:T(8,128)}, f32[4,8,32,128]{3,2,1,0:T(8,128)S(1)}, u32[]{:S(2)}) copy-start(f32[4,8,32,128]{3,2,1,0:T(8,128)S(1)} %copy.596) | copy-start | bytes 1572868
  96.7 33.4 %copy-start.147 = (f32[32]{0:T(128)S(1)}, f32[32]{0:T(128)}, u32[]{:S(2)}) copy-start(f32[32]{0:T(128)} %param.14) | copy-start | bytes 388
  96.8 33.4 %copy-start.149 = (f32[32]{0:T(128)S(1)}, f32[32]{0:T(128)}, u32[]{:S(2)}) copy-start(f32[32]{0:T(128)} %param.13) | copy-start | bytes 388
  130.1 12.6 %copy-start.102 = (bf16[3,3,3,32,32]{4,3,2,1,0:T(8,128)(2,1)S(1)}, bf16[3,3,3,32,32]{4,3,2,1,0:T(8,128)(2,1)}, u32[]{:S(2)}) copy-start(bf16[3,3,3,32,32]{4,3,2,1,0:T(8,128)(2,1)} %param.12) | copy-start | bytes 165892
  130.1 12.6 %copy-start.103 = (bf16[3,3,3,32,32]{3,4,2,1,0:T(8,128)(2,1)S(1)}, bf16[3,3,3,32,32]{3,4,2,1,0:T(8,128)(2,1)}, u32[]{:S(2)}) copy-start(bf16[3,3,3,32,32]{3,4,2,1,0:T(8,128)(2,1)} %reverse_bitcast_fusion) | copy-start | bytes 165892
  130.7 13.4 %collective-permute-start.6 = (bf16[2,32,1,16,128]{4,3,2,1,0:T(8,128)(2,1)S(1)}, bf16[2,32,1,16,128]{4,3,2,1,0:T(8,128)(2,1)S(1)}, u32[]{:S(2)}, u32[]{:S(2)}) collective-permute-start(bf16[2,32,1,16,128]{4,3,2,1,0:T(8,128)(2,1)S(1)} %get-tuple-element.257), channel_id=1, source_target_pairs={{0,32},{32,64},{64,96},{1,33},{33,65},{65,97},{2,34},{34,66},{66,9... | collective-permute-start | bytes 786440 | tf_op jit(solution)/shard_map/ppermute | solution.py:24
  140.7 9.2 %collective-permute-start.7 = (bf16[2,32,1,16,128]{4,3,2,1,0:T(8,128)(2,1)S(1)}, bf16[2,32,1,16,128]{4,3,2,1,0:T(8,128)(2,1)S(1)}, u32[]{:S(2)}, u32[]{:S(2)}) collective-permute-start(bf16[2,32,1,16,128]{4,3,2,1,0:T(8,128)(2,1)S(1)} %get-tuple-element.258), channel_id=1, source_target_pairs={{32,0},{64,32},{96,64},{33,1},{65,33},{97,65},{34,2},{66,34},{98,6... | collective-permute-start | bytes 786440 | tf_op jit(solution)/shard_map/ppermute | solution.py:27
  156.6 10.6 %copy-start.126 = (bf16[32,3,32]{2,0,1:T(8,128)(2,1)S(1)}, bf16[32,3,32]{2,0,1:T(8,128)(2,1)}, u32[]{:S(2)}) copy-start(bf16[32,3,32]{2,0,1:T(8,128)(2,1)} %get-tuple-element.292) | copy-start | bytes 18436
  156.6 10.7 %copy-start.125 = (bf16[32,3,32]{2,0,1:T(8,128)(2,1)S(1)}, bf16[32,3,32]{2,0,1:T(8,128)(2,1)}, u32[]{:S(2)}) copy-start(bf16[32,3,32]{2,0,1:T(8,128)(2,1)} %get-tuple-element.293) | copy-start | bytes 18436
  156.6 10.9 %copy-start.124 = (bf16[32,3,32]{2,0,1:T(8,128)(2,1)S(1)}, bf16[32,3,32]{2,0,1:T(8,128)(2,1)}, u32[]{:S(2)}) copy-start(bf16[32,3,32]{2,0,1:T(8,128)(2,1)} %get-tuple-element.294) | copy-start | bytes 18436
  156.6 11.0 %copy-start.123 = (bf16[32,3,32]{2,0,1:T(8,128)(2,1)S(1)}, bf16[32,3,32]{2,0,1:T(8,128)(2,1)}, u32[]{:S(2)}) copy-start(bf16[32,3,32]{2,0,1:T(8,128)(2,1)} %get-tuple-element.295) | copy-start | bytes 18436
  156.6 11.1 %copy-start.122 = (bf16[32,3,32]{2,0,1:T(8,128)(2,1)S(1)}, bf16[32,3,32]{2,0,1:T(8,128)(2,1)}, u32[]{:S(2)}) copy-start(bf16[32,3,32]{2,0,1:T(8,128)(2,1)} %get-tuple-element.296) | copy-start | bytes 18436
  156.6 11.2 %copy-start.121 = (bf16[32,3,32]{2,0,1:T(8,128)(2,1)S(1)}, bf16[32,3,32]{2,0,1:T(8,128)(2,1)}, u32[]{:S(2)}) copy-start(bf16[32,3,32]{2,0,1:T(8,128)(2,1)} %get-tuple-element.297) | copy-start | bytes 18436
  158.7 9.2 %collective-permute-start.8 = (bf16[2,32,4,1,128]{1,2,4,3,0:T(4,128)(2,1)}, bf16[2,32,4,1,128]{1,2,4,3,0:T(4,128)(2,1)S(1)}, u32[]{:S(2)}, u32[]{:S(2)}) collective-permute-start(bf16[2,32,4,1,128]{1,2,4,3,0:T(4,128)(2,1)} %get-tuple-element.77), channel_id=1, source_target_pairs={{0,8},{8,16},{16,24},{1,9},{9,17},{17,25},{2,10},{10,18},{18,26},{... | collective-permute-start | bytes 196616 | tf_op jit(solution)/shard_map/ppermute | solution.py:24
  160.9 7.4 %collective-permute-start.9 = (bf16[2,32,4,1,128]{1,2,4,3,0:T(4,128)(2,1)}, bf16[2,32,4,1,128]{1,2,4,3,0:T(4,128)(2,1)}, u32[]{:S(2)}, u32[]{:S(2)}) collective-permute-start(bf16[2,32,4,1,128]{1,2,4,3,0:T(4,128)(2,1)} %get-tuple-element.78), channel_id=1, source_target_pairs={{8,0},{16,8},{24,16},{9,1},{17,9},{25,17},{10,2},{18,10},{26,18},{... | collective-permute-start | bytes 196616 | tf_op jit(solution)/shard_map/ppermute | solution.py:27
  168.0 12.0 %copy-start.146 = (f32[2,32]{1,0:T(2,128)S(1)}, f32[2,32]{1,0:T(2,128)}, u32[]{:S(2)}) copy-start(f32[2,32]{1,0:T(2,128)} %copy-done.145) | copy-start | bytes 772
  168.0 12.0 %copy-start.150 = (f32[32]{0:T(128)S(1)}, f32[32]{0:T(128)}, u32[]{:S(2)}) copy-start(f32[32]{0:T(128)} %param.13) | copy-start | bytes 388
  176.8 23.2 %collective-permute-start.10 = (bf16[2,32,4,18,1]{1,2,4,3,0:T(4,128)(2,1)S(1)}, bf16[2,32,4,18,1]{1,2,4,3,0:T(4,128)(2,1)S(1)}, u32[]{:S(2)}, u32[]{:S(2)}) collective-permute-start(bf16[2,32,4,18,1]{1,2,4,3,0:T(4,128)(2,1)S(1)} %get-tuple-element.73), channel_id=1, source_target_pairs={{0,1},{1,2},{2,3},{3,4},{4,5},{5,6},{6,7},{8,9},{9,10},{10,11},{11... | collective-permute-start | bytes 27656 | tf_op jit(solution)/shard_map/ppermute | solution.py:24
  178.6 20.5 %collective-permute-start.11 = (bf16[2,32,4,18,1]{1,2,4,3,0:T(4,128)(2,1)S(1)}, bf16[2,32,4,18,1]{1,2,4,3,0:T(4,128)(2,1)S(1)}, u32[]{:S(2)}, u32[]{:S(2)}) collective-permute-start(bf16[2,32,4,18,1]{1,2,4,3,0:T(4,128)(2,1)S(1)} %get-tuple-element.74), channel_id=1, source_target_pairs={{1,0},{2,1},{3,2},{4,3},{5,4},{6,5},{7,6},{9,8},{10,9},{11,10},{12... | collective-permute-start | bytes 27656 | tf_op jit(solution)/shard_map/ppermute | solution.py:27
  181.2 3.4 copy-start.3
  239.1 3.4 copy-start.61
  239.2 3.4 copy-start.62
  245.2 3.5 copy-start.56
  245.2 3.5 copy-start.57
  253.4 29.2 %copy-start.152 = (f32[32]{0:T(128)S(1)}, f32[32]{0:T(128)}, u32[]{:S(2)}) copy-start(f32[32]{0:T(128)} %param.15) | copy-start | bytes 388
  253.4 29.3 %copy-start.106 = (bf16[32,2,16,128]{3,2,1,0:T(8,128)(2,1)S(1)}, bf16[32,2,16,128]{3,2,1,0:T(8,128)(2,1)}, u32[]{:S(2)}) copy-start(bf16[32,2,16,128]{3,2,1,0:T(8,128)(2,1)} %param.17) | copy-start | bytes 786436
  253.4 29.3 %copy-start.151 = (f32[32]{0:T(128)S(1)}, f32[32]{0:T(128)}, u32[]{:S(2)}) copy-start(f32[32]{0:T(128)} %param.16) | copy-start | bytes 388
  254.0 28.8 %copy-start.43 = (f32[4,8,32,128]{3,2,1,0:T(8,128)S(1)}, f32[4,8,32,128]{3,2,1,0:T(8,128)}, u32[]{:S(2)}) copy-start(f32[4,8,32,128]{3,2,1,0:T(8,128)} %copy.606) | copy-start | bytes 1572868
  316.8 14.5 %copy-start.33 = (bf16[3,32,4096]{2,1,0:T(8,128)(2,1)S(1)}, bf16[3,32,4096]{2,1,0:T(8,128)(2,1)}, u32[]{:S(2)}) copy-start(bf16[3,32,4096]{2,1,0:T(8,128)(2,1)} %dot_general.398) | copy-start | bytes 2359300
  318.1 13.9 %copy-start.36 = (bf16[3,32,4096]{2,1,0:T(8,128)(2,1)S(1)}, bf16[3,32,4096]{2,1,0:T(8,128)(2,1)}, u32[]{:S(2)}) copy-start(bf16[3,32,4096]{2,1,0:T(8,128)(2,1)} %dot_general.400) | copy-start | bytes 2359300
  318.2 18.2 %collective-permute-start.12 = (bf16[32,1,16,128]{3,0,2,1:T(8,128)(2,1)}, bf16[32,1,16,128]{3,0,2,1:T(8,128)(2,1)S(1)}, u32[]{:S(2)}, u32[]{:S(2)}) collective-permute-start(bf16[32,1,16,128]{3,0,2,1:T(8,128)(2,1)} %get-tuple-element.269), channel_id=1, source_target_pairs={{0,32},{32,64},{64,96},{1,33},{33,65},{65,97},{2,34},{34,66},{66,9... | collective-permute-start | bytes 393224 | tf_op jit(solution)/shard_map/ppermute | solution.py:24
  327.6 5.0 copy-start.40
  327.6 8.8 %collective-permute-start.13 = (bf16[32,1,16,128]{3,0,2,1:T(8,128)(2,1)S(1)}, bf16[32,1,16,128]{3,0,2,1:T(8,128)(2,1)S(1)}, u32[]{:S(2)}, u32[]{:S(2)}) collective-permute-start(bf16[32,1,16,128]{3,0,2,1:T(8,128)(2,1)S(1)} %get-tuple-element.270), channel_id=1, source_target_pairs={{32,0},{64,32},{96,64},{33,1},{65,33},{97,65},{34,2},{66,34},{98,6... | collective-permute-start | bytes 393224 | tf_op jit(solution)/shard_map/ppermute | solution.py:27
  335.1 6.8 %copy-start.97 = (bf16[32,2,16,128]{3,0,2,1:T(8,128)(2,1)S(1)}, bf16[32,2,16,128]{3,0,2,1:T(8,128)(2,1)}, u32[]{:S(2)}) copy-start(bf16[32,2,16,128]{3,0,2,1:T(8,128)(2,1)} %get-tuple-element.307) | copy-start | bytes 786436
  336.4 6.3 %collective-permute-start.14 = (bf16[32,4,1,128]{3,0,2,1:T(8,128)(2,1)S(1)}, bf16[32,4,1,128]{3,0,2,1:T(8,128)(2,1)S(1)}, u32[]{:S(2)}, u32[]{:S(2)}) collective-permute-start(bf16[32,4,1,128]{3,0,2,1:T(8,128)(2,1)S(1)} %get-tuple-element.255), channel_id=1, source_target_pairs={{0,8},{8,16},{16,24},{1,9},{9,17},{17,25},{2,10},{10,18},{18,26},{... | collective-permute-start | bytes 98312 | tf_op jit(solution)/shard_map/ppermute | solution.py:24
  339.8 4.7 collective-permute-start.15
  342.8 9.3 %copy-start.104 = (bf16[32,4,1,128]{3,0,2,1:T(8,128)(2,1)}, bf16[32,4,1,128]{3,0,2,1:T(8,128)(2,1)S(1)}, u32[]{:S(2)}) copy-start(bf16[32,4,1,128]{3,0,2,1:T(8,128)(2,1)S(1)} %collective-permute-done.14) | copy-start | bytes 98308
  344.5 7.6 %copy-start.105 = (bf16[32,4,1,128]{3,0,2,1:T(8,128)(2,1)}, bf16[32,4,1,128]{3,0,2,1:T(8,128)(2,1)S(1)}, u32[]{:S(2)}) copy-start(bf16[32,4,1,128]{3,0,2,1:T(8,128)(2,1)S(1)} %collective-permute-done.15) | copy-start | bytes 98308
  346.7 7.0 %collective-permute-start.17 = (bf16[32,4,18,1]{0,2,3,1:T(8,128)(2,1)S(1)}, bf16[32,4,18,1]{0,2,3,1:T(8,128)(2,1)}, u32[]{:S(2)}, u32[]{:S(2)}) collective-permute-start(bf16[32,4,18,1]{0,2,3,1:T(8,128)(2,1)S(1)} %copy.531), channel_id=1, source_target_pairs={{1,0},{2,1},{3,2},{4,3},{5,4},{6,5},{7,6},{9,8},{10,9},{11,10},{12... | collective-permute-start | bytes 13832 | tf_op jit(solution)/shard_map/ppermute | solution.py:27
  348.0 5.1 collective-permute-start.16
  366.1 31.5 %copy-start.22 = (f32[4,8,32,128]{3,2,1,0:T(8,128)S(1)}, f32[4,8,32,128]{3,2,1,0:T(8,128)}, u32[]{:S(2)}) copy-start(f32[4,8,32,128]{3,2,1,0:T(8,128)} %copy-done.21) | copy-start | bytes 1572868
  397.3 13.6 %copy-start.28 = (bf16[3,32,4096]{2,1,0:T(8,128)(2,1)S(1)}, bf16[3,32,4096]{2,1,0:T(8,128)(2,1)}, u32[]{:S(2)}) copy-start(bf16[3,32,4096]{2,1,0:T(8,128)(2,1)} %dot_general.378) | copy-start | bytes 2359300
  397.5 14.0 %copy-start.29 = (bf16[3,32,4096]{2,1,0:T(8,128)(2,1)S(1)}, bf16[3,32,4096]{2,1,0:T(8,128)(2,1)}, u32[]{:S(2)}) copy-start(bf16[3,32,4096]{2,1,0:T(8,128)(2,1)} %dot_general.380) | copy-start | bytes 2359300
  398.3 13.9 %copy-start.30 = (bf16[3,32,4096]{2,1,0:T(8,128)(2,1)S(1)}, bf16[3,32,4096]{2,1,0:T(8,128)(2,1)}, u32[]{:S(2)}) copy-start(bf16[3,32,4096]{2,1,0:T(8,128)(2,1)} %dot_general.382) | copy-start | bytes 2359300
  398.3 19.1 %collective-permute-start.18 = (bf16[32,1,16,128]{3,0,2,1:T(8,128)(2,1)S(1)}, bf16[32,1,16,128]{3,0,2,1:T(8,128)(2,1)S(1)}, u32[]{:S(2)}, u32[]{:S(2)}) collective-permute-start(bf16[32,1,16,128]{3,0,2,1:T(8,128)(2,1)S(1)} %get-tuple-element.264), channel_id=1, source_target_pairs={{0,32},{32,64},{64,96},{1,33},{33,65},{65,97},{2,34},{34,66},{66,9... | collective-permute-start | bytes 393224 | tf_op jit(solution)/shard_map/ppermute | solution.py:24
  408.7 4.1 copy-start.32
  408.7 8.7 %collective-permute-start.19 = (bf16[32,1,16,128]{3,0,2,1:T(8,128)(2,1)S(1)}, bf16[32,1,16,128]{3,0,2,1:T(8,128)(2,1)S(1)}, u32[]{:S(2)}, u32[]{:S(2)}) collective-permute-start(bf16[32,1,16,128]{3,0,2,1:T(8,128)(2,1)S(1)} %get-tuple-element.265), channel_id=1, source_target_pairs={{32,0},{64,32},{96,64},{33,1},{65,33},{97,65},{34,2},{66,34},{98,6... | collective-permute-start | bytes 393224 | tf_op jit(solution)/shard_map/ppermute | solution.py:27
  417.4 5.5 collective-permute-start.20
  421.1 4.7 collective-permute-start.21
  427.4 6.8 %collective-permute-start.23 = (bf16[32,4,18,1]{0,2,3,1:T(8,128)(2,1)S(1)}, bf16[32,4,18,1]{0,2,3,1:T(8,128)(2,1)S(1)}, u32[]{:S(2)}, u32[]{:S(2)}) collective-permute-start(bf16[32,4,18,1]{0,2,3,1:T(8,128)(2,1)S(1)} %copy.546), channel_id=1, source_target_pairs={{1,0},{2,1},{3,2},{4,3},{5,4},{6,5},{7,6},{9,8},{10,9},{11,10},{12... | collective-permute-start | bytes 13832 | tf_op jit(solution)/shard_map/ppermute | solution.py:27
  428.7 4.9 collective-permute-start.22
  (114 other events, 149.4 us)
Sparse Core Ops, SparseCore 0:
  417.5 145.4 all-reduce.22
where the time goes:
time: 580 us; the launch traced here: 574 us
  waiting for transfers between devices  142 us (24%)
  local copies, waits for them, and re-layouts  139 us (24%)
  blocking collectives  119 us (21%)
  starting transfers between devices  80.6 us (14%)
  other arithmetic  40.1 us (7%)
  matrix products  36.2 us (6%)
  between operations  17.5 us (3%)
    psum x20, blocking collectives, by_axis(): return functools.reduce(lax.psum, axes, value)  119 us
    psum x1, waiting for transfers between devices, body(): grad_w_first = lax.psum(local_first, GX_GY_GZ)  118 us
    ppermute x12, starting transfers between devices, extended(): lax.ppermute(lax.slice_in_dim(block, block.shape[dim] - width, None, axis...  62 us
    dot_general x18, local copies, waits for them, and re-layouts, kernel_grad(): lax.dot_general(flat, stacked, (((1,), (1,)), ((), ())), preferred_elemen...  25.1 us
    dot_general x54, matrix products, convolve(): total = total + jnp.dot(matrix, stacked, preferred_element_type=jnp.float32)  24.7 us
    unnamed x315, local copies, waits for them, and re-layouts  23.5 us
    concatenate x4, local copies, waits for them, and re-layouts, extended(): block = jnp.concatenate([low, block, high], axis=dim)  22.8 us
    concatenate x12, other arithmetic, extended(): block = jnp.concatenate([low, block, high], axis=dim)  21.5 us
  transfers between devices with their start and end apart: 25, of which 12 were waited for; matrix products, arithmetic and copies ran while one was open for 12% of the time, Pallas kernels for 0%

commit v1 on v0

--- a/solution.py
+++ b/solution.py
@@ -155,7 +155,7 @@
     local_first = kernel_grad(input_pad_b, delta_one) * factor
     delta_pad_one = extended(delta_one, ((GX, 1), ("gy", 2), (GZ, 3)), 1)
     dx_b = convolve(delta_pad_one, flipped(w_first)).astype(jnp.bfloat16)
-    grad_w_first = lax.psum(local_first, GX_GY_GZ)
+    grad_w_first = jnp.sum(lax.all_gather(local_first, GX_GY_GZ), axis=0)
     grad_norm = jnp.stack([sum_x1, sum_d1, sum_x2, sum_d2]) * factor
     return (y_a, dx_b, grad_w_first, grad_w_second, grad_norm)
 

time: 580 us -> 925 us (1.59)
  waiting for transfers between devices: 142 us -> 484 us
  other arithmetic: 40.1 us -> 62 us
    all_gather x0 -> x1, waiting for transfers between devices: none -> 309 us  [body(): grad_w_first = jnp.sum(lax.all_gather(local_first, GX_GY_GZ), axis=0)]
    reduce_sum x0 -> x1, other arithmetic: none -> 18.9 us  [body(): grad_w_first = jnp.sum(lax.all_gather(local_first, GX_GY_GZ), axis=0)]
    ppermute x12, waiting for transfers between devices: 20.6 us -> 38 us  [extended(): lax.ppermute(lax.slice_in_dim(block, 0, width, axis=dim), axis, backward)]
    psum x1, waiting for transfers between devices: 118 us -> 130 us  [body(): grad_w_second = lax.psum(local_second, GX_GY_GZ)]
    unnamed x315 -> x306, local copies, waits for them, and re-layouts: 23.5 us -> 29.9 us
  transfers between devices with their start and end apart: 25 -> 26, of which waited for: 12 -> 16; matrix products, arithmetic and copies ran while one was open for 12% -> 10% of each run, Pallas kernels for 0% -> 0%
where the time goes in v1:
time: 925 us; the launch traced here: 919 us
  waiting for transfers between devices  484 us (52%)
  local copies, waits for them, and re-layouts  131 us (14%)
  blocking collectives  114 us (12%)
  starting transfers between devices  74.1 us (8%)
  other arithmetic  62 us (7%)
  matrix products  36.6 us (4%)
  between operations  17.4 us (2%)
    all_gather x1, waiting for transfers between devices, body(): grad_w_first = jnp.sum(lax.all_gather(local_first, GX_GY_GZ), axis=0)  309 us
    psum x1, waiting for transfers between devices, body(): grad_w_second = lax.psum(local_second, GX_GY_GZ)  130 us
    psum x20, blocking collectives, by_axis(): return functools.reduce(lax.psum, axes, value)  114 us
    ppermute x12, starting transfers between devices, extended(): lax.ppermute(lax.slice_in_dim(block, block.shape[dim] - width, None, axis...  55.4 us
    ppermute x12, waiting for transfers between devices, extended(): lax.ppermute(lax.slice_in_dim(block, 0, width, axis=dim), axis, backward)  38 us
    unnamed x306, local copies, waits for them, and re-layouts  29.9 us
    dot_general x54, matrix products, convolve(): total = total + jnp.dot(matrix, stacked, preferred_element_type=jnp.float32)  25 us
    concatenate x4, local copies, waits for them, and re-layouts, extended(): block = jnp.concatenate([low, block, high], axis=dim)  23.1 us
  transfers between devices with their start and end apart: 26, of which 16 were waited for; matrix products, arithmetic and copies ran while one was open for 10% of the time, Pallas kernels for 0%

profile of v1, /device:TPU:1, one launch (start us, length us, event | category | flops | bytes accessed | tf_op | source)
XLA Modules:
  0.0 918.8 jit_solution(8349542820634315366)
XLA Ops:
  8.4 6.9 collective-permute-start
  15.3 1.9 collective-permute-start.1
  18.6 5.9 collective-permute-done.1
  25.6 3.7 copy.460
  30.6 3.1 collective-permute-start.2
  35.2 1.8 collective-permute-done.2
  37.0 4.0 collective-permute-done.3
  41.0 6.2 pad_maximum_fusion
  47.2 2.2 copy-done
  49.4 2.6 collective-permute-start.4
  58.6 6.3 copy.464
  70.3 2.3 fusion.176
  72.6 3.0 fusion.175
  98.3 5.3 all-reduce.19
  103.6 2.5 all-reduce.15
  106.0 7.2 all-reduce.7
  113.2 11.0 %all-reduce.3 = (f32[2,32]{1,0:T(2,128)S(1)}, f32[2,32]{1,0:T(2,128)S(1)}) all-reduce(f32[2,32]{1,0:T(2,128)S(1)} %get-tuple-element.43, f32[2,32]{1,0:T(2,128)S(1)} %get-tuple-element.44), channel_id=1, replica_groups=mesh['gx_0'=2,'gx_1'=2,'gy'=4,'gz_0'=4,'gz_1'=2] {'gz_0'}, use_global_device_ids=true, to_apply=%region_12.0 | all-reduce | flops 128 | bytes 1024 | tf_op jit(solution)/shard_map/psum | solution.py:16
  124.1 3.8 all-reduce.11
  131.2 10.1 %collective-permute-start.6 = (bf16[2,32,1,16,128]{4,3,2,1,0:T(8,128)(2,1)S(1)}, bf16[2,32,1,16,128]{4,3,2,1,0:T(8,128)(2,1)S(1)}, u32[]{:S(2)}, u32[]{:S(2)}) collective-permute-start(bf16[2,32,1,16,128]{4,3,2,1,0:T(8,128)(2,1)S(1)} %get-tuple-element.255), channel_id=1, source_target_pairs={{0,32},{32,64},{64,96},{1,33},{33,65},{65,97},{2,34},{34,66},{66,9... | collective-permute-start | bytes 786440 | tf_op jit(solution)/shard_map/ppermute | solution.py:24
  141.3 1.9 collective-permute-start.7
  144.6 5.9 collective-permute-done.7
  151.6 5.6 copy.493
  158.5 2.2 collective-permute-start.8
  162.0 1.9 collective-permute-done.8
  164.0 3.8 collective-permute-done.9
  167.8 6.2 pad_maximum_fusion.1
  174.0 2.2 copy-done.1
  176.2 2.3 collective-permute-start.10
  181.6 7.4 copy.497
  189.0 2.0 copy.496
  191.0 2.0 copy.498
  192.9 3.3 pad_maximum_fusion.3
  198.1 3.2 fusion.171
  212.2 1.9 copy.606
  230.2 5.3 all-reduce.18
  235.4 2.5 all-reduce.14
  237.9 6.0 all-reduce.6
  243.9 8.0 all-reduce.2
  251.9 3.8 all-reduce.10
  257.6 2.9 fusion.162
  260.5 5.3 all-reduce.17
  265.8 8.6 all-reduce.13
  274.4 7.4 all-reduce.5
  281.8 6.2 all-reduce.1
  288.0 4.0 all-reduce.9
  294.1 10.3 %collective-permute-start.12 = (bf16[32,1,16,128]{3,0,2,1:T(8,128)(2,1)S(1)}, bf16[32,1,16,128]{3,0,2,1:T(8,128)(2,1)S(1)}, u32[]{:S(2)}, u32[]{:S(2)}) collective-permute-start(bf16[32,1,16,128]{3,0,2,1:T(8,128)(2,1)S(1)} %get-tuple-element.267), channel_id=1, source_target_pairs={{0,32},{32,64},{64,96},{1,33},{33,65},{65,97},{2,34},{34,66},{66,9... | collective-permute-start | bytes 393224 | tf_op jit(solution)/shard_map/ppermute | solution.py:24
  304.4 1.9 collective-permute-start.13
  307.9 4.3 collective-permute-done.13
  329.9 3.1 collective-permute-start.16
  352.3 5.4 all-reduce.16
  357.7 2.5 all-reduce.12
  360.2 8.2 all-reduce.4
  368.4 7.1 all-reduce
  375.5 4.2 all-reduce.8
  396.7 1.9 copy.576
  406.4 9.2 %collective-permute-start.18 = (bf16[32,1,16,128]{3,0,2,1:T(8,128)(2,1)S(1)}, bf16[32,1,16,128]{3,0,2,1:T(8,128)(2,1)S(1)}, u32[]{:S(2)}, u32[]{:S(2)}) collective-permute-start(bf16[32,1,16,128]{3,0,2,1:T(8,128)(2,1)S(1)} %get-tuple-element.262), channel_id=1, source_target_pairs={{0,32},{32,64},{64,96},{1,33},{33,65},{65,97},{2,34},{34,66},{66,9... | collective-permute-start | bytes 393224 | tf_op jit(solution)/shard_map/ppermute | solution.py:24
  415.7 1.9 collective-permute-start.19
  418.9 5.9 collective-permute-done.19
  428.1 3.4 collective-permute-done.21
  432.6 2.5 collective-permute-start.22
  437.9 3.1 collective-permute-done.23
  452.2 308.9 %all-gather.2.cloned.1.call-done = f32[128,3,3,3,32,32]{5,4,3,2,1,0:T(8,128)} async-done(((f32[1,3,3,3,32,32]{5,4,3,2,1,0:T(8,128)}), f32[128,3,3,3,32,32]{5,4,3,2,1,0:T(8,128)}) %all-gather.2.cloned.1.call-update) | async-done | bytes 14155792 | tf_op jit(solution)/shard_map/all_gather | solution.py:158
  761.1 18.9 %reduce_sum.129 = f32[3,3,3,32,32]{4,3,2,1,0:T(8,128)} reduce(f32[128,3,3,3,32,32]{5,4,3,2,1,0:T(8,128)} %all-gather.2.cloned.1.call-done, f32[]{:T(128)} %constant.15.clone.1), dimensions={0}, to_apply=%region_52.53 | reduce | flops 3511296 | bytes 14266372 | tf_op jit(solution)/shard_map/reduce_sum | solution.py:158
  780.0 130.0 %all-reduce.22.cloned.1.call-done = f32[3,3,3,32,32]{4,3,2,1,0:T(8,128)} async-done(((f32[3,3,3,32,32]{4,3,2,1,0:T(8,128)}), f32[3,3,3,32,32]{4,3,2,1,0:T(8,128)}) %all-reduce.22.cloned.1.call-update) | async-done | bytes 110608 | tf_op jit(solution)/shard_map/psum | solution.py:149
  (634 shorter events, 167.6 us)
Async XLA Ops:
  7.2 754.0 %all-gather.2.cloned.1.call-start = ((), (), s32[]{:S(2)}) async-start(), calls=%async_computation | async-start | bytes 57065472 | tf_op jit(solution)/shard_map/all_gather | solution.py:158
  8.4 10.2 %collective-permute-start = (bf16[2,32,1,16,128]{4,3,2,1,0:T(8,128)(2,1)S(1)}, bf16[2,32,1,16,128]{4,3,2,1,0:T(8,128)(2,1)S(1)}, u32[]{:S(2)}, u32[]{:S(2)}) collective-permute-start(bf16[2,32,1,16,128]{4,3,2,1,0:T(8,128)(2,1)S(1)} %get-tuple-element.257), channel_id=1, source_target_pairs={{0,32},{32,64},{64,96},{1,33},{33,65},{65,97},{2,34},{34,66},{66,9... | collective-permute-start | bytes 786440 | tf_op jit(solution)/shard_map/ppermute | solution.py:24
  15.3 9.2 %collective-permute-start.1 = (bf16[2,32,1,16,128]{4,3,2,1,0:T(8,128)(2,1)S(1)}, bf16[2,32,1,16,128]{4,3,2,1,0:T(8,128)(2,1)S(1)}, u32[]{:S(2)}, u32[]{:S(2)}) collective-permute-start(bf16[2,32,1,16,128]{4,3,2,1,0:T(8,128)(2,1)S(1)} %get-tuple-element.258), channel_id=1, source_target_pairs={{32,0},{64,32},{96,64},{33,1},{65,33},{97,65},{34,2},{66,34},{98,6... | collective-permute-start | bytes 786440 | tf_op jit(solution)/shard_map/ppermute | solution.py:27
  30.6 6.4 collective-permute-start.2
  33.7 19.6 %copy-start.99 = (bf16[3,3,3,32,32]{4,3,2,1,0:T(8,128)(2,1)S(1)}, bf16[3,3,3,32,32]{4,3,2,1,0:T(8,128)(2,1)}, u32[]{:S(2)}) copy-start(bf16[3,3,3,32,32]{4,3,2,1,0:T(8,128)(2,1)} %param.11) | copy-start | bytes 165892
  33.7 7.2 collective-permute-start.3
  49.4 15.5 %collective-permute-start.4 = (bf16[2,32,4,18,1]{1,2,4,3,0:T(4,128)(2,1)S(1)}, bf16[2,32,4,18,1]{1,2,4,3,0:T(4,128)(2,1)S(1)}, u32[]{:S(2)}, u32[]{:S(2)}) collective-permute-start(bf16[2,32,4,18,1]{1,2,4,3,0:T(4,128)(2,1)S(1)} %get-tuple-element.73), channel_id=1, source_target_pairs={{0,1},{1,2},{2,3},{3,4},{4,5},{5,6},{6,7},{8,9},{9,10},{10,11},{11... | collective-permute-start | bytes 27656 | tf_op jit(solution)/shard_map/ppermute | solution.py:24
  52.0 13.8 %collective-permute-start.5 = (bf16[2,32,4,18,1]{1,2,4,3,0:T(4,128)(2,1)S(1)}, bf16[2,32,4,18,1]{1,2,4,3,0:T(4,128)(2,1)}, u32[]{:S(2)}, u32[]{:S(2)}) collective-permute-start(bf16[2,32,4,18,1]{1,2,4,3,0:T(4,128)(2,1)S(1)} %get-tuple-element.74), channel_id=1, source_target_pairs={{1,0},{2,1},{3,2},{4,3},{5,4},{6,5},{7,6},{9,8},{10,9},{11,10},{12... | collective-permute-start | bytes 27656 | tf_op jit(solution)/shard_map/ppermute | solution.py:27
  77.2 3.2 copy-start.2
  77.6 3.4 copy-start.4
  78.0 3.3 copy-start.6
  78.3 3.5 copy-start.8
  78.8 3.4 copy-start.10
  79.1 3.5 copy-start.12
  95.7 33.9 %copy-start.127 = (f32[32]{0:T(128)S(1)}, f32[32]{0:T(128)}, u32[]{:S(2)}) copy-start(f32[32]{0:T(128)} %param.14) | copy-start | bytes 388
  95.7 33.9 %copy-start.130 = (f32[32]{0:T(128)S(1)}, f32[32]{0:T(128)}, u32[]{:S(2)}) copy-start(f32[32]{0:T(128)} %param.13) | copy-start | bytes 388
  128.0 3.3 copy-start.119
  128.5 2.7 copy-start.122
  131.2 13.4 %collective-permute-start.6 = (bf16[2,32,1,16,128]{4,3,2,1,0:T(8,128)(2,1)S(1)}, bf16[2,32,1,16,128]{4,3,2,1,0:T(8,128)(2,1)S(1)}, u32[]{:S(2)}, u32[]{:S(2)}) collective-permute-start(bf16[2,32,1,16,128]{4,3,2,1,0:T(8,128)(2,1)S(1)} %get-tuple-element.255), channel_id=1, source_target_pairs={{0,32},{32,64},{64,96},{1,33},{33,65},{65,97},{2,34},{34,66},{66,9... | collective-permute-start | bytes 786440 | tf_op jit(solution)/shard_map/ppermute | solution.py:24
  141.3 9.2 %collective-permute-start.7 = (bf16[2,32,1,16,128]{4,3,2,1,0:T(8,128)(2,1)S(1)}, bf16[2,32,1,16,128]{4,3,2,1,0:T(8,128)(2,1)S(1)}, u32[]{:S(2)}, u32[]{:S(2)}) collective-permute-start(bf16[2,32,1,16,128]{4,3,2,1,0:T(8,128)(2,1)S(1)} %get-tuple-element.256), channel_id=1, source_target_pairs={{32,0},{64,32},{96,64},{33,1},{65,33},{97,65},{34,2},{66,34},{98,6... | collective-permute-start | bytes 786440 | tf_op jit(solution)/shard_map/ppermute | solution.py:27
  151.6 10.4 %copy-start.98 = (bf16[3,3,3,32,32]{4,3,2,1,0:T(8,128)(2,1)S(1)}, bf16[3,3,3,32,32]{4,3,2,1,0:T(8,128)(2,1)}, u32[]{:S(2)}) copy-start(bf16[3,3,3,32,32]{4,3,2,1,0:T(8,128)(2,1)} %param.12) | copy-start | bytes 165892
  158.5 5.5 collective-permute-start.8
  160.7 7.1 collective-permute-start.9
  176.2 12.8 %collective-permute-start.10 = (bf16[2,32,4,18,1]{1,2,4,3,0:T(4,128)(2,1)S(1)}, bf16[2,32,4,18,1]{1,2,4,3,0:T(4,128)(2,1)S(1)}, u32[]{:S(2)}, u32[]{:S(2)}) collective-permute-start(bf16[2,32,4,18,1]{1,2,4,3,0:T(4,128)(2,1)S(1)} %get-tuple-element.71), channel_id=1, source_target_pairs={{0,1},{1,2},{2,3},{3,4},{4,5},{5,6},{6,7},{8,9},{9,10},{10,11},{11... | collective-permute-start | bytes 27656 | tf_op jit(solution)/shard_map/ppermute | solution.py:24
  178.6 12.4 %collective-permute-start.11 = (bf16[2,32,4,18,1]{1,2,4,3,0:T(4,128)(2,1)S(1)}, bf16[2,32,4,18,1]{1,2,4,3,0:T(4,128)(2,1)S(1)}, u32[]{:S(2)}, u32[]{:S(2)}) collective-permute-start(bf16[2,32,4,18,1]{1,2,4,3,0:T(4,128)(2,1)S(1)} %get-tuple-element.72), channel_id=1, source_target_pairs={{1,0},{2,1},{3,2},{4,3},{5,4},{6,5},{7,6},{9,8},{10,9},{11,10},{12... | collective-permute-start | bytes 27656 | tf_op jit(solution)/shard_map/ppermute | solution.py:27
  215.7 11.9 %copy-start.14 = (bf16[96,2,16,128]{3,2,1,0:T(8,128)(2,1)}, bf16[96,2,16,128]{3,2,1,0:T(8,128)(2,1)S(1)}, u32[]{:S(2)}) copy-start(bf16[96,2,16,128]{3,2,1,0:T(8,128)(2,1)S(1)} %copy.525) | copy-start | bytes 2359300
  216.2 11.0 %copy-start.16 = (bf16[96,2,16,128]{3,2,1,0:T(8,128)(2,1)}, bf16[96,2,16,128]{3,2,1,0:T(8,128)(2,1)S(1)}, u32[]{:S(2)}) copy-start(bf16[96,2,16,128]{3,2,1,0:T(8,128)(2,1)S(1)} %copy.524) | copy-start | bytes 2359300
  217.7 9.1 copy-start.18
  218.8 7.5 copy-start.20
  219.9 6.0 copy-start.22
  221.0 4.5 copy-start.24
  222.1 2.9 copy-start.26
  227.6 29.2 %copy-start.148 = (f32[32]{0:T(128)S(1)}, f32[32]{0:T(128)}, u32[]{:S(2)}) copy-start(f32[32]{0:T(128)} %param.15) | copy-start | bytes 388
  227.6 30.0 %copy-start.102 = (bf16[32,2,16,128]{3,2,1,0:T(8,128)(2,1)S(1)}, bf16[32,2,16,128]{3,2,1,0:T(8,128)(2,1)}, u32[]{:S(2)}) copy-start(bf16[32,2,16,128]{3,2,1,0:T(8,128)(2,1)} %param.17) | copy-start | bytes 786436
  227.6 30.0 %copy-start.147 = (f32[32]{0:T(128)S(1)}, f32[32]{0:T(128)}, u32[]{:S(2)}) copy-start(f32[32]{0:T(128)} %param.16) | copy-start | bytes 388
  260.5 55.6 %copy-start.126 = (f32[2,32]{1,0:T(2,128)S(1)}, f32[2,32]{1,0:T(2,128)}, u32[]{:S(2)}) copy-start(f32[2,32]{1,0:T(2,128)} %copy-done.125) | copy-start | bytes 772
  260.5 55.7 %copy-start.131 = (f32[32]{0:T(128)S(1)}, f32[32]{0:T(128)}, u32[]{:S(2)}) copy-start(f32[32]{0:T(128)} %param.13) | copy-start | bytes 388
  294.1 13.8 %collective-permute-start.12 = (bf16[32,1,16,128]{3,0,2,1:T(8,128)(2,1)S(1)}, bf16[32,1,16,128]{3,0,2,1:T(8,128)(2,1)S(1)}, u32[]{:S(2)}, u32[]{:S(2)}) collective-permute-start(bf16[32,1,16,128]{3,0,2,1:T(8,128)(2,1)S(1)} %get-tuple-element.267), channel_id=1, source_target_pairs={{0,32},{32,64},{64,96},{1,33},{33,65},{65,97},{2,34},{34,66},{66,9... | collective-permute-start | bytes 393224 | tf_op jit(solution)/shard_map/ppermute | solution.py:24
  304.4 7.8 collective-permute-start.13
  312.8 15.0 %collective-permute-start.14 = (bf16[32,4,1,128]{3,0,2,1:T(8,128)(2,1)}, bf16[32,4,1,128]{3,0,2,1:T(8,128)(2,1)S(1)}, u32[]{:S(2)}, u32[]{:S(2)}) collective-permute-start(bf16[32,4,1,128]{3,0,2,1:T(8,128)(2,1)} %get-tuple-element.253), channel_id=1, source_target_pairs={{0,8},{8,16},{16,24},{1,9},{9,17},{17,25},{2,10},{10,18},{18,26},{... | collective-permute-start | bytes 98312 | tf_op jit(solution)/shard_map/ppermute | solution.py:24
  314.6 13.2 %collective-permute-start.15 = (bf16[32,4,1,128]{3,0,2,1:T(8,128)(2,1)}, bf16[32,4,1,128]{3,0,2,1:T(8,128)(2,1)S(1)}, u32[]{:S(2)}, u32[]{:S(2)}) collective-permute-start(bf16[32,4,1,128]{3,0,2,1:T(8,128)(2,1)} %get-tuple-element.254), channel_id=1, source_target_pairs={{8,0},{16,8},{24,16},{9,1},{17,9},{25,17},{10,2},{18,10},{26,18},{... | collective-permute-start | bytes 98312 | tf_op jit(solution)/shard_map/ppermute | solution.py:27
  320.3 2.5 copy-start.7
  321.6 2.5 copy-start.9
  329.9 6.0 collective-permute-start.16
  333.6 4.6 collective-permute-start.17
  350.8 29.4 %copy-start.133 = (f32[32]{0:T(128)S(1)}, f32[32]{0:T(128)}, u32[]{:S(2)}) copy-start(f32[32]{0:T(128)} %fusion.159) | copy-start | bytes 388
  350.9 29.6 %copy-start.41 = (bf16[3,32,4096]{2,1,0:T(8,128)(2,1)S(1)}, bf16[3,32,4096]{2,1,0:T(8,128)(2,1)}, u32[]{:S(2)}) copy-start(bf16[3,32,4096]{2,1,0:T(8,128)(2,1)} %dot_general.378) | copy-start | bytes 2359300
  352.3 28.8 %copy-start.42 = (bf16[3,32,4096]{2,1,0:T(8,128)(2,1)S(1)}, bf16[3,32,4096]{2,1,0:T(8,128)(2,1)}, u32[]{:S(2)}) copy-start(bf16[3,32,4096]{2,1,0:T(8,128)(2,1)} %dot_general.380) | copy-start | bytes 2359300
  386.9 523.1 %all-reduce.22.cloned.1.call-start = ((), (), s32[]{:S(2)}) async-start(), calls=%async_computation.1 | async-start | bytes 884736 | tf_op jit(solution)/shard_map/psum | solution.py:149
  387.7 2.5 copy-start.27
  389.0 2.5 copy-start.25
  396.7 3.7 copy-start.47
  396.7 4.3 copy-start.46
  398.6 3.1 copy-start.45
  405.6 21.8 %copy-start.140 = (f32[32]{0:T(128)S(1)}, f32[32]{0:T(128)}, u32[]{:S(2)}) copy-start(f32[32]{0:T(128)} %copy-done.139) | copy-start | bytes 388
  405.6 21.8 %copy-start.142 = (f32[32]{0:T(128)S(1)}, f32[32]{0:T(128)}, u32[]{:S(2)}) copy-start(f32[32]{0:T(128)} %copy-done.141) | copy-start | bytes 388
  405.6 21.8 %copy-start.144 = (f32[32]{0:T(128)S(1)}, f32[32]{0:T(128)}, u32[]{:S(2)}) copy-start(f32[32]{0:T(128)} %copy-done.143) | copy-start | bytes 388
  405.7 21.8 %copy-start.146 = (f32[32]{0:T(128)S(1)}, f32[32]{0:T(128)}, u32[]{:S(2)}) copy-start(f32[32]{0:T(128)} %copy-done.145) | copy-start | bytes 388
  406.4 12.5 %collective-permute-start.18 = (bf16[32,1,16,128]{3,0,2,1:T(8,128)(2,1)S(1)}, bf16[32,1,16,128]{3,0,2,1:T(8,128)(2,1)S(1)}, u32[]{:S(2)}, u32[]{:S(2)}) collective-permute-start(bf16[32,1,16,128]{3,0,2,1:T(8,128)(2,1)S(1)} %get-tuple-element.262), channel_id=1, source_target_pairs={{0,32},{32,64},{64,96},{1,33},{33,65},{65,97},{2,34},{34,66},{66,9... | collective-permute-start | bytes 393224 | tf_op jit(solution)/shard_map/ppermute | solution.py:24
  415.7 9.2 collective-permute-start.19
  424.8 3.2 collective-permute-start.20
  426.1 5.3 collective-permute-start.21
  432.6 4.7 collective-permute-start.22
  435.8 5.2 collective-permute-start.23
  (111 other events, 139.8 us)
Sparse Core Ops, SparseCore 0:
  387.0 374.0 all-gather.1
  765.9 144.0 all-reduce.21
